TPU v7x, 32 devices: a whole 2x2x4 slice. The times are simulated.
32 devices in a mesh: unit: 4 (over y, x), replica: 2 (over core), model: 4 (over z).
Axes of the slice: x: 2, y: 2, z: 4, core: 2. Of those that a mesh axis runs over, the one named last changes fastest.
Arguments:
- slope_up: float32 [8, 768, 3072], P(('unit', 'replica'), None, 'model'), parts along dimension 0, may hold values from -0.875 to 0.875
- slope_down: float32 [8, 3072, 768], P(('unit', 'replica'), 'model'), parts along dimension 0, may hold values from -0.875 to 0.875
- slope_query: float32 [8, 768, 768], P(('unit', 'replica'), None, 'model'), parts along dimension 0, may hold values from -0.875 to 0.875
- slope_key: float32 [8, 768, 768], P(('unit', 'replica'), None, 'model'), parts along dimension 0, may hold values from -0.875 to 0.875
- slope_value: float32 [8, 768, 768], P(('unit', 'replica'), None, 'model'), parts along dimension 0, may hold values from -0.875 to 0.875
- slope_mixed: float32 [8, 768, 768], P(('unit', 'replica'), 'model'), parts along dimension 0, may hold values from -0.875 to 0.875
- slope_norm: float32 [8, 768], P(('unit', 'replica')), parts along dimension 0, may hold values from -8 to 8
- param_up: float32 [3072, 3072], P(('unit', 'replica'), 'model'), parts along dimension 0, may hold values from -0.21875 to 0.21875
- param_down: float32 [12288, 768], P(('unit', 'model'), 'replica'), parts along dimension 0, may hold values from -0.109375 to 0.109375
- param_query: float32 [3072, 768], P(('unit', 'replica'), 'model'), parts along dimension 0, may hold values from -0.21875 to 0.21875
- param_key: float32 [3072, 768], P(('unit', 'replica'), 'model'), parts along dimension 0, may hold values from -0.21875 to 0.21875
- param_value: float32 [3072, 768], P(('unit', 'replica'), 'model'), parts along dimension 0, may hold values from -0.21875 to 0.21875
- param_mixed: float32 [3072, 768], P(('unit', 'model'), 'replica'), parts along dimension 0, may hold values from -0.21875 to 0.21875
- param_norm: float32 [3072], P(('unit', 'replica')), parts along dimension 0, may hold values from 0.25 to 1.75
Outputs:
- half_up: bfloat16 [3072, 3072], P('unit', 'model'), parts along dimension 0
- half_down: bfloat16 [12288, 768], P(('unit', 'model')), parts along dimension 0
- half_query: bfloat16 [3072, 768], P('unit', 'model'), parts along dimension 0
- half_key: bfloat16 [3072, 768], P('unit', 'model'), parts along dimension 0
- half_value: bfloat16 [3072, 768], P('unit', 'model'), parts along dimension 0
- half_mixed: bfloat16 [3072, 768], P(('unit', 'model')), parts along dimension 0
- half_norm: bfloat16 [3072], P('unit'), parts along dimension 0
- next_up: float32 [3072, 3072], P(('unit', 'replica'), 'model'), parts along dimension 0
- next_down: float32 [12288, 768], P(('unit', 'model'), 'replica'), parts along dimension 0
- next_query: float32 [3072, 768], P(('unit', 'replica'), 'model'), parts along dimension 0
- next_key: float32 [3072, 768], P(('unit', 'replica'), 'model'), parts along dimension 0
- next_value: float32 [3072, 768], P(('unit', 'replica'), 'model'), parts along dimension 0
- next_mixed: float32 [3072, 768], P(('unit', 'model'), 'replica'), parts along dimension 0
- next_norm: float32 [3072], P(('unit', 'replica')), parts along dimension 0
There are 4 independent parts, one for each index of `unit`. A program takes and returns all parts, laid end to end along the dimension named above; each array names one. Nothing has to cross between parts.
All inputs are finite; a program needn't handle non-finite values.
Results may differ from a plain program's by a relative error of at most 0.001.
Values may be sent and summed in bfloat16 or wider, within the bound.
A program may use at most 64 MiB of HBM per device.

v0:
```python
import jax
import jax.numpy as jnp
from jax import lax
from jax.sharding import PartitionSpec as P

learn_rate = 0.3


def shards(
    slope_up,
    slope_down,
    slope_query,
    slope_key,
    slope_value,
    slope_mixed,
    slope_norm,
    param_up,
    param_down,
    param_query,
    param_key,
    param_value,
    param_mixed,
    param_norm,
):
    mean_up, mean_down, mean_query, mean_key, mean_value, mean_mixed = (
        lax.psum_scatter(slope_up[0], "replica", scatter_dimension=0, tiled=True),
        lax.psum_scatter(slope_down[0], "replica", scatter_dimension=1, tiled=True),
        lax.psum_scatter(slope_query[0], "replica", scatter_dimension=0, tiled=True),
        lax.psum_scatter(slope_key[0], "replica", scatter_dimension=0, tiled=True),
        lax.psum_scatter(slope_value[0], "replica", scatter_dimension=0, tiled=True),
        lax.psum_scatter(slope_mixed[0], "replica", scatter_dimension=1, tiled=True),
    )
    whole_norm = lax.psum(slope_norm[0], "replica")
    place = lax.axis_index("replica")
    mean_norm = lax.dynamic_slice_in_dim(
        whole_norm, place * param_norm.shape[0], param_norm.shape[0]
    )
    mean_rate = lax.axis_size("replica") ** (-0.5)
    mean_up = mean_up * mean_rate
    mean_down = mean_down * mean_rate
    mean_query = mean_query * mean_rate
    mean_key = mean_key * mean_rate
    mean_value = mean_value * mean_rate
    mean_mixed = mean_mixed * mean_rate
    mean_norm = mean_norm * mean_rate
    next_up = param_up - learn_rate * mean_up
    next_down = param_down - learn_rate * mean_down
    next_query = param_query - learn_rate * mean_query
    next_key = param_key - learn_rate * mean_key
    next_value = param_value - learn_rate * mean_value
    next_mixed = param_mixed - learn_rate * mean_mixed
    next_norm = param_norm - learn_rate * mean_norm
    half_up, half_down, half_query, half_key, half_value, half_mixed, half_norm = (
        lax.all_gather(next_up.astype(jnp.bfloat16), "replica", axis=0, tiled=True),
        lax.all_gather(next_down.astype(jnp.bfloat16), "replica", axis=1, tiled=True),
        lax.all_gather(next_query.astype(jnp.bfloat16), "replica", axis=0, tiled=True),
        lax.all_gather(next_key.astype(jnp.bfloat16), "replica", axis=0, tiled=True),
        lax.all_gather(next_value.astype(jnp.bfloat16), "replica", axis=0, tiled=True),
        lax.all_gather(next_mixed.astype(jnp.bfloat16), "replica", axis=1, tiled=True),
        lax.all_gather(next_norm.astype(jnp.bfloat16), "replica", axis=0, tiled=True),
    )
    return (
        half_up,
        half_down,
        half_query,
        half_key,
        half_value,
        half_mixed,
        half_norm,
        next_up,
        next_down,
        next_query,
        next_key,
        next_value,
        next_mixed,
        next_norm,
    )


def solution(mesh):
    placed = (
        P(("unit", "replica"), None, "model"),
        P(("unit", "replica"), "model", None),
        P(("unit", "replica"), None, "model"),
        P(("unit", "replica"), None, "model"),
        P(("unit", "replica"), None, "model"),
        P(("unit", "replica"), "model", None),
        P(("unit", "replica"), None),
        P(("unit", "replica"), "model"),
        P(("unit", "model"), "replica"),
        P(("unit", "replica"), "model"),
        P(("unit", "replica"), "model"),
        P(("unit", "replica"), "model"),
        P(("unit", "model"), "replica"),
        P(("unit", "replica")),
    )
    return jax.shard_map(
        shards,
        mesh=mesh,
        in_specs=placed,
        out_specs=(
            P("unit", "model"),
            P(("unit", "model"), None),
            P("unit", "model"),
            P("unit", "model"),
            P("unit", "model"),
            P(("unit", "model"), None),
            P("unit"),
            P(("unit", "replica"), "model"),
            P(("unit", "model"), "replica"),
            P(("unit", "replica"), "model"),
            P(("unit", "replica"), "model"),
            P(("unit", "replica"), "model"),
            P(("unit", "model"), "replica"),
            P(("unit", "replica")),
        ),
        check_vma=False,
    )
```

profile of v0, /device:TPU:3, one launch (start us, length us, event | category | flops | bytes accessed | tf_op | source)
XLA Modules:
  0.0 119.3 jit_solution(7985728365988198458)
XLA Ops:
  7.2 0.0 reduce-scatter.7.cloned.1.call-start
  7.2 0.7 reduce-scatter.7.cloned.1.call-update
  7.9 0.0 reduce-scatter.9.cloned.1.call-start
  8.0 0.7 reduce-scatter.9.cloned.1.call-update
  8.7 0.0 reduce-scatter.11.cloned.1.call-start
  8.7 0.0 copy-start.1
  8.7 0.7 reduce-scatter.11.cloned.1.call-update
  9.4 0.0 reduce-scatter.13.cloned.1.call-start
  9.4 0.5 reduce-scatter.13.cloned.1.call-update
  10.0 0.0 reduce-scatter.15.cloned.1.call-start
  10.0 0.5 reduce-scatter.15.cloned.1.call-update
  10.6 0.0 reduce-scatter.17.cloned.1.call-start
  10.6 0.5 reduce-scatter.17.cloned.1.call-update
  11.1 0.0 copy-start.7
  11.1 0.0 copy-start.8
  11.2 0.0 all-gather.4.cloned.1.call-start
  11.2 11.1 %reduce-scatter.7.cloned.1.call-done = f32[384,768]{1,0:T(8,128)} async-done(((f32[768,768]{1,0:T(8,128)}), f32[384,768]{1,0:T(8,128)}) %reduce-scatter.7.cloned.1.call-update) | async-done | bytes 1179664 | tf_op jit(solution)/shard_map/reduce_scatter | solution.py:26
  22.3 0.0 copy-done.1
  22.3 0.0 copy-start.2
  22.3 2.7 %fusion.6 = (bf16[384,768]{1,0:T(8,128)(2,1)}, f32[384,768]{1,0:T(8,128)}) fusion(f32[384,768]{1,0:T(8,128)S(1)} %copy-done.1, f32[384,768]{1,0:T(8,128)} %reduce-scatter.7.cloned.1.call-done), kind=kLoop, calls=%fused_computation.13 | loop fusion | flops 884736 | bytes 4128768 | tf_op jit(solution)/shard_map/convert_element_type | solution.py:54
  25.0 0.0 all-gather.4.cloned.1.call-update
  25.1 0.0 all-gather.6.cloned.1.call-start
  25.1 0.0 copy-done.7
  25.1 2.5 %psum.7 = f32[768]{0:T(1024)S(1)} all-reduce(f32[768]{0:T(1024)S(1)} %reduce), channel_id=1, replica_groups=mesh['unit'=4,'replica'=2,'model'=4] {'replica'}, use_global_device_ids=true, to_apply=%region_6.0 | all-reduce | flops 768 | bytes 6144 | tf_op jit(solution)/shard_map/psum | solution.py:33
  27.6 0.0 copy-done.8
  27.6 0.7 fusion
  28.3 1.8 %all-gather = bf16[2,1,384]{2,1,0:T(2,128)(2,1)S(1)} all-gather(bf16[1,1,384]{2,1,0:T(2,128)(2,1)S(1)} %reshape.28), channel_id=1, replica_groups=mesh['unit'=4,'replica'=2,'model'=4] {'replica'}, dimensions={0}, use_global_device_ids=true | all-gather | bytes 2304 | tf_op jit(solution)/shard_map/all_gather | solution.py:60
  30.1 0.6 reshape.29
  30.7 0.0 copy-start.3
  30.7 5.1 %reduce-scatter.9.cloned.1.call-done = f32[768,384]{1,0:T(8,128)} async-done(((f32[768,768]{1,0:T(8,128)}), f32[768,384]{1,0:T(8,128)}) %reduce-scatter.9.cloned.1.call-update) | async-done | bytes 1179664 | tf_op jit(solution)/shard_map/reduce_scatter | solution.py:27
  35.8 0.0 copy-done.2
  35.8 2.6 %fusion.5 = (bf16[768,384]{1,0:T(8,128)(2,1)}, f32[768,384]{1,0:T(8,128)}) fusion(f32[768,384]{1,0:T(8,128)S(1)} %copy-done.2, f32[768,384]{1,0:T(8,128)} %reduce-scatter.9.cloned.1.call-done), kind=kLoop, calls=%fused_computation.12 | loop fusion | flops 884736 | bytes 4128768 | tf_op jit(solution)/shard_map/convert_element_type | solution.py:55
  38.4 0.0 copy-start.4
  38.5 0.0 all-gather.6.cloned.1.call-update
  38.5 8.9 %reduce-scatter.11.cloned.1.call-done = f32[384,192]{0,1:T(8,128)} async-done(((f32[768,192]{0,1:T(8,128)}), f32[384,192]{0,1:T(8,128)}) %reduce-scatter.11.cloned.1.call-update) | async-done | bytes 294928 | tf_op jit(solution)/shard_map/reduce_scatter | solution.py:28
  47.4 0.0 copy-done.3
  47.4 1.7 %fusion.4 = (bf16[384,192]{0,1:T(8,128)(2,1)S(1)}, f32[384,192]{0,1:T(8,128)}) fusion(f32[384,192]{0,1:T(8,128)S(1)} %copy-done.3, f32[384,192]{0,1:T(8,128)} %reduce-scatter.11.cloned.1.call-done), kind=kLoop, calls=%fused_computation.11 | loop fusion | flops 221184 | bytes 1032192 | tf_op jit(solution)/shard_map/convert_element_type | solution.py:56
  49.1 0.0 copy-start.5
  49.1 2.1 %all_gather.23 = bf16[768,192]{0,1:T(8,128)(2,1)S(1)} all-gather(bf16[384,192]{0,1:T(8,128)(2,1)S(1)} %get-tuple-element.22), channel_id=1, replica_groups=mesh['unit'=4,'replica'=2,'model'=4] {'replica'}, dimensions={0}, use_global_device_ids=true | all-gather | bytes 442368 | tf_op jit(solution)/shard_map/all_gather | solution.py:56
  51.3 7.4 %reduce-scatter.13.cloned.1.call-done = f32[384,192]{0,1:T(8,128)} async-done(((f32[768,192]{0,1:T(8,128)}), f32[384,192]{0,1:T(8,128)}) %reduce-scatter.13.cloned.1.call-update) | async-done | bytes 294928 | tf_op jit(solution)/shard_map/reduce_scatter | solution.py:29
  58.7 0.0 copy-done.4
  58.7 1.7 %fusion.3 = (bf16[384,192]{0,1:T(8,128)(2,1)S(1)}, f32[384,192]{0,1:T(8,128)}) fusion(f32[384,192]{0,1:T(8,128)S(1)} %copy-done.4, f32[384,192]{0,1:T(8,128)} %reduce-scatter.13.cloned.1.call-done), kind=kLoop, calls=%fused_computation.10 | loop fusion | flops 221184 | bytes 1032192 | tf_op jit(solution)/shard_map/convert_element_type | solution.py:57
  60.4 0.0 copy-start.6
  60.4 2.1 %all_gather.24 = bf16[768,192]{0,1:T(8,128)(2,1)S(1)} all-gather(bf16[384,192]{0,1:T(8,128)(2,1)S(1)} %get-tuple-element.20), channel_id=1, replica_groups=mesh['unit'=4,'replica'=2,'model'=4] {'replica'}, dimensions={0}, use_global_device_ids=true | all-gather | bytes 442368 | tf_op jit(solution)/shard_map/all_gather | solution.py:57
  62.5 7.4 %reduce-scatter.15.cloned.1.call-done = f32[384,192]{0,1:T(8,128)} async-done(((f32[768,192]{0,1:T(8,128)}), f32[384,192]{0,1:T(8,128)}) %reduce-scatter.15.cloned.1.call-update) | async-done | bytes 294928 | tf_op jit(solution)/shard_map/reduce_scatter | solution.py:30
  69.9 0.0 copy-done.5
  69.9 1.7 %fusion.2 = (bf16[384,192]{0,1:T(8,128)(2,1)S(1)}, f32[384,192]{0,1:T(8,128)}) fusion(f32[384,192]{0,1:T(8,128)S(1)} %copy-done.5, f32[384,192]{0,1:T(8,128)} %reduce-scatter.15.cloned.1.call-done), kind=kLoop, calls=%fused_computation.9 | loop fusion | flops 221184 | bytes 1032192 | tf_op jit(solution)/shard_map/convert_element_type | solution.py:58
  71.6 2.0 %all_gather.25 = bf16[768,192]{0,1:T(8,128)(2,1)S(1)} all-gather(bf16[384,192]{0,1:T(8,128)(2,1)S(1)} %get-tuple-element.18), channel_id=1, replica_groups=mesh['unit'=4,'replica'=2,'model'=4] {'replica'}, dimensions={0}, use_global_device_ids=true | all-gather | bytes 442368 | tf_op jit(solution)/shard_map/all_gather | solution.py:58
  73.6 7.5 %reduce-scatter.17.cloned.1.call-done = f32[192,384]{1,0:T(8,128)} async-done(((f32[192,768]{1,0:T(8,128)}), f32[192,384]{1,0:T(8,128)}) %reduce-scatter.17.cloned.1.call-update) | async-done | bytes 294928 | tf_op jit(solution)/shard_map/reduce_scatter | solution.py:31
  81.2 0.0 copy-done.6
  81.2 1.7 %fusion.1 = (bf16[192,384]{1,0:T(8,128)(2,1)S(1)}, f32[192,384]{1,0:T(8,128)}) fusion(f32[192,384]{1,0:T(8,128)S(1)} %copy-done.6, f32[192,384]{1,0:T(8,128)} %reduce-scatter.17.cloned.1.call-done), kind=kLoop, calls=%fused_computation.8 | loop fusion | flops 221184 | bytes 1032192 | tf_op jit(solution)/shard_map/convert_element_type | solution.py:59
  82.9 2.0 %all_gather.26 = bf16[192,768]{1,0:T(8,128)(2,1)S(1)} all-gather(bf16[192,384]{1,0:T(8,128)(2,1)S(1)} %get-tuple-element.16), channel_id=1, replica_groups=mesh['unit'=4,'replica'=2,'model'=4] {'replica'}, dimensions={1}, use_global_device_ids=true | all-gather | bytes 442368 | tf_op jit(solution)/shard_map/all_gather | solution.py:59
  84.9 8.8 %all-gather.4.cloned.1.call-done = bf16[768,768]{1,0:T(8,128)(2,1)} async-done(((bf16[384,768]{1,0:T(8,128)(2,1)}), bf16[768,768]{1,0:T(8,128)(2,1)}) %all-gather.4.cloned.1.call-update) | async-done | bytes 1179664 | tf_op jit(solution)/shard_map/all_gather | solution.py:54
  93.7 12.5 %all-gather.6.cloned.1.call-done = bf16[768,768]{1,0:T(8,128)(2,1)} async-done(((bf16[768,384]{1,0:T(8,128)(2,1)}), bf16[768,768]{1,0:T(8,128)(2,1)}) %all-gather.6.cloned.1.call-update) | async-done | bytes 1179664 | tf_op jit(solution)/shard_map/all_gather | solution.py:55
  106.2 0.0 copy-start
  106.2 2.5 %copy.34 = bf16[768,768]{1,0:T(8,128)(2,1)} copy(bf16[768,768]{1,0:T(8,128)(2,1)} %all-gather.4.cloned.1.call-done) | data formatting | bytes 2359296
  108.6 0.0 copy-done
  108.6 1.0 copy.35
  109.7 0.7 copy.36
  110.4 0.7 copy.37
  111.1 0.7 copy.38
  111.8 0.7 copy.39
  (3 shorter events, 0.0 us)
Async XLA Ops:
  7.2 15.1 %reduce-scatter.7.cloned.1.call-start = ((), (), s32[]{:S(2)}) async-start(), calls=%async_computation.6 | async-start | bytes 3538944 | tf_op jit(solution)/shard_map/reduce_scatter | solution.py:26
  7.9 27.9 %reduce-scatter.9.cloned.1.call-start = ((), (), s32[]{:S(2)}) async-start(), calls=%async_computation.8 | async-start | bytes 3538944 | tf_op jit(solution)/shard_map/reduce_scatter | solution.py:27
  8.7 38.8 %reduce-scatter.11.cloned.1.call-start = ((), (), s32[]{:S(2)}) async-start(), calls=%async_computation.10 | async-start | bytes 884736 | tf_op jit(solution)/shard_map/reduce_scatter | solution.py:28
  8.7 13.6 %copy-start.1 = (f32[384,768]{1,0:T(8,128)S(1)}, f32[384,768]{1,0:T(8,128)}, u32[]{:S(2)}) copy-start(f32[384,768]{1,0:T(8,128)} %param.21) | copy-start | bytes 3538948
  9.4 49.3 %reduce-scatter.13.cloned.1.call-start = ((), (), s32[]{:S(2)}) async-start(), calls=%async_computation.11 | async-start | bytes 884736 | tf_op jit(solution)/shard_map/reduce_scatter | solution.py:29
  10.0 59.9 %reduce-scatter.15.cloned.1.call-start = ((), (), s32[]{:S(2)}) async-start(), calls=%async_computation.12 | async-start | bytes 884736 | tf_op jit(solution)/shard_map/reduce_scatter | solution.py:30
  10.6 70.6 %reduce-scatter.17.cloned.1.call-start = ((), (), s32[]{:S(2)}) async-start(), calls=%async_computation.13 | async-start | bytes 884736 | tf_op jit(solution)/shard_map/reduce_scatter | solution.py:31
  11.1 14.0 %copy-start.7 = (f32[1,768]{1,0:T(1,128)S(1)}, f32[1,768]{1,0:T(1,128)}, u32[]{:S(2)}) copy-start(f32[1,768]{1,0:T(1,128)} %param.20) | copy-start | bytes 9220
  11.1 16.5 %copy-start.8 = (f32[384]{0:T(512)S(1)}, f32[384]{0:T(512)}, u32[]{:S(2)}) copy-start(f32[384]{0:T(512)} %param.27) | copy-start | bytes 4612
  11.2 82.5 %all-gather.4.cloned.1.call-start = ((), (), s32[]{:S(2)}) async-start(), calls=%async_computation.7 | async-start | bytes 1769472 | tf_op jit(solution)/shard_map/all_gather | solution.py:54
  22.3 13.5 %copy-start.2 = (f32[768,384]{1,0:T(8,128)S(1)}, f32[768,384]{1,0:T(8,128)}, u32[]{:S(2)}) copy-start(f32[768,384]{1,0:T(8,128)} %param.22) | copy-start | bytes 3538948
  25.1 81.1 %all-gather.6.cloned.1.call-start = ((), (), s32[]{:S(2)}) async-start(), calls=%async_computation.9 | async-start | bytes 1769472 | tf_op jit(solution)/shard_map/all_gather | solution.py:55
  30.7 16.7 %copy-start.3 = (f32[384,192]{0,1:T(8,128)S(1)}, f32[384,192]{0,1:T(8,128)}, u32[]{:S(2)}) copy-start(f32[384,192]{0,1:T(8,128)} %param.23) | copy-start | bytes 884740
  38.4 20.2 %copy-start.4 = (f32[384,192]{0,1:T(8,128)S(1)}, f32[384,192]{0,1:T(8,128)}, u32[]{:S(2)}) copy-start(f32[384,192]{0,1:T(8,128)} %param.24) | copy-start | bytes 884740
  49.1 20.8 %copy-start.5 = (f32[384,192]{0,1:T(8,128)S(1)}, f32[384,192]{0,1:T(8,128)}, u32[]{:S(2)}) copy-start(f32[384,192]{0,1:T(8,128)} %param.25) | copy-start | bytes 884740
  60.4 20.8 %copy-start.6 = (f32[192,384]{1,0:T(8,128)S(1)}, f32[192,384]{1,0:T(8,128)}, u32[]{:S(2)}) copy-start(f32[192,384]{1,0:T(8,128)} %param.26) | copy-start | bytes 884740
  106.2 2.5 %copy-start = (bf16[768,768]{1,0:T(8,128)(2,1)S(1)}, bf16[768,768]{1,0:T(8,128)(2,1)}, u32[]{:S(2)}) copy-start(bf16[768,768]{1,0:T(8,128)(2,1)} %all-gather.6.cloned.1.call-done) | copy-start | bytes 3538948
Sparse Core Ops, SparseCore 0:
  10.2 12.0 reduce-scatter.6
  24.5 11.2 reduce-scatter.8
  38.1 9.2 reduce-scatter.10
  49.5 9.0 reduce-scatter.12
  60.8 9.0 reduce-scatter.14
  72.0 9.0 reduce-scatter.16
  83.3 10.3 all-gather.3
  95.8 10.3 all-gather.5
where the time goes:
time: 121 us; the launch traced here: 119 us
  waiting for transfers between devices  72.4 us (60%)
  between operations  14.2 us (12%)
  other arithmetic  12.9 us (11%)
  blocking collectives  12.6 us (10%)
  local copies, waits for them, and re-layouts  6.96 us (6%)
    all_gather x1, waiting for transfers between devices, shards(): lax.all_gather(next_down.astype(jnp.bfloat16), 'replica', axis=1, tiled=T...  12.5 us
    reduce_scatter x1, waiting for transfers between devices, shards(): lax.psum_scatter(slope_up[0], 'replica', scatter_dimension=0, tiled=True)  11.1 us
    reduce_scatter x1, waiting for transfers between devices, shards(): lax.psum_scatter(slope_query[0], 'replica', scatter_dimension=0, tiled=True)  8.94 us
    all_gather x1, waiting for transfers between devices, shards(): lax.all_gather(next_up.astype(jnp.bfloat16), 'replica', axis=0, tiled=True)  8.76 us
    reduce_scatter x1, waiting for transfers between devices, shards(): lax.psum_scatter(slope_mixed[0], 'replica', scatter_dimension=1, tiled=True)  7.54 us
    reduce_scatter x1, waiting for transfers between devices, shards(): lax.psum_scatter(slope_key[0], 'replica', scatter_dimension=0, tiled=True)  7.4 us
    reduce_scatter x1, waiting for transfers between devices, shards(): lax.psum_scatter(slope_value[0], 'replica', scatter_dimension=0, tiled=True)  7.39 us
    unnamed x26, local copies, waits for them, and re-layouts  6.96 us
  transfers between devices with their start and end apart: 8, of which 8 were waited for; matrix products, arithmetic and copies ran while one was open for 11% of the time, Pallas kernels for 0%

commit v1 on v0

--- a/solution.py
+++ b/solution.py
@@ -1,12 +1,223 @@
+import functools
+
 import jax
 import jax.numpy as jnp
 from jax import lax
+from jax.experimental import pallas as pl
+from jax.experimental.pallas import tpu as pltpu
 from jax.sharding import PartitionSpec as P
 
 learn_rate = 0.3
-
-
-def shards(
+ANY = pl.BlockSpec(memory_space=pl.ANY)
+VMEM_BYTES = 67043328
+
+
+def pieces(shape, split_rows, parts):
+    rows = shape[0]
+    if rows % (16 * parts):
+        parts = 1
+    return [(part * (rows // parts), rows // parts) for part in range(parts)]
+
+
+def plan(halves, by_row, small):
+    chunks = []
+    for at, half in enumerate(halves):
+        parts = max(1, half[0] * half[1] // small)
+        chunks += [(at, start, rows) for start, rows in pieces(half, by_row[at], parts)]
+    return chunks
+
+
+def exchange(n, by_row, chunks, rate, *refs):
+    m = len(by_row)
+    slopes, slope_norm = refs[:m], refs[m]
+    params, param_norm = refs[m + 1 : 2 * m + 1], refs[2 * m + 1]
+    refs = refs[2 * m + 2 :]
+    halfs, norm_half = refs[:m], refs[m]
+    kept, norm_next = refs[m + 1 : 2 * m + 1], refs[2 * m + 1]
+    refs = refs[2 * m + 2 :]
+    own, got = refs[:m], refs[m : 2 * m]
+    (norms, norm_kept, in_sem, keep_sem, send_sem, recv_sem,
+     back_send, back_recv, norm_in, norm_send, norm_recv) = refs[2 * m :]
+
+    me = lax.axis_index("replica")
+    peer = 1 - me
+    there = {"replica": peer}
+
+    def half_of(at, who, start, rows):
+        height, width = kept[at].shape
+        if by_row[at]:
+            return pl.ds(pl.multiple_of(who * height + start, 16), rows), pl.ds(0, width)
+        return pl.ds(start, rows), pl.ds(pl.multiple_of(who * width, width), width)
+
+    def remote(source, target, out_sem, in_sem):
+        return pltpu.make_async_remote_copy(
+            src_ref=source,
+            dst_ref=target,
+            send_sem=out_sem,
+            recv_sem=in_sem,
+            device_id=there,
+            device_id_type=pl.DeviceIdType.MESH,
+        )
+
+    loads = []
+    for c, (at, start, rows) in enumerate(chunks):
+        mine = pl.ds(start, rows)
+        loads.append((
+            pltpu.make_async_copy(
+                slopes[at].at[(0, *half_of(at, me, start, rows))], own[at].at[mine], in_sem.at[c]
+            ),
+            pltpu.make_async_copy(params[at].at[mine], kept[at].at[mine], keep_sem.at[c]),
+        ))
+    norm_loads = (
+        pltpu.make_async_copy(slope_norm, norms.at[pl.ds(me, 1)], norm_in.at[0]),
+        pltpu.make_async_copy(param_norm, norm_kept.at[pl.ds(me, 1)], norm_in.at[1]),
+    )
+
+    barrier = pltpu.get_barrier_semaphore()
+    pl.semaphore_signal(barrier, inc=1, device_id=there, device_id_type=pl.DeviceIdType.MESH)
+    pl.semaphore_wait(barrier, 1)
+
+    norm_sends = [
+        remote(slope_norm, norms.at[pl.ds(me, 1)], norm_send.at[0], norm_recv.at[0]),
+        remote(param_norm, norm_kept.at[pl.ds(me, 1)], norm_send.at[1], norm_recv.at[1]),
+    ]
+    sends = [
+        remote(
+            slopes[at].at[(0, *half_of(at, peer, start, rows))],
+            got[at].at[pl.ds(start, rows)],
+            send_sem.at[c],
+            recv_sem.at[c],
+        )
+        for c, (at, start, rows) in enumerate(chunks)
+    ]
+    for send in sends + norm_sends:
+        send.start()
+    for load in loads:
+        load[0].start()
+        load[1].start()
+    for load in norm_loads:
+        load.start()
+
+    backs = []
+    for c, (at, start, rows) in enumerate(chunks):
+        loads[c][0].wait()
+        loads[c][1].wait()
+        sends[c].wait_recv()
+        step = 32 if rows % 32 == 0 else 16
+        height, width = kept[at].shape
+
+        @pl.loop(0, rows // step)
+        def update(block, at=at, start=start, step=step, height=height, width=width):
+            first = pl.multiple_of(start + block * step, step)
+            span = pl.ds(first, step)
+            mean = (own[at][span] + got[at][span]) * rate
+            moved = kept[at][span] - learn_rate * mean
+            kept[at][span] = moved
+            halfs[at][half_of(at, me, first, step)] = moved.astype(jnp.bfloat16)
+
+        place = half_of(at, me, start, rows)
+        back = remote(halfs[at].at[place], halfs[at].at[place], back_send.at[c], back_recv.at[c])
+        back.start()
+        backs.append(back)
+
+    for load in norm_loads:
+        load.wait()
+    for send in norm_sends:
+        send.wait_recv()
+    width = norm_kept.shape[1]
+    for who in range(n):
+        cut = pl.ds(who * width, width)
+        total = norms[0:1, cut]
+        for other in range(1, n):
+            total += norms[other : other + 1, cut]
+        moved = norm_kept[who : who + 1] - learn_rate * (total * rate)
+        norm_half[0:1, cut] = moved
+
+        @pl.when(who == me)
+        def keep():
+            norm_next[...] = moved
+
+    for send in sends + norm_sends:
+        send.wait_send()
+    for back in backs:
+        back.wait()
+
+
+def settle(count, *refs):
+    sems = refs[-1]
+    copies = [
+        pltpu.make_async_copy(refs[k], refs[count + k], sems.at[k]) for k in range(count)
+    ]
+    for copy in copies:
+        copy.start()
+    for copy in copies:
+        copy.wait()
+
+
+def shards(n, *arrays):
+    m = len(arrays) // 2 - 1
+    slopes, slope_norm = list(arrays[:m]), arrays[m]
+    params, param_norm = list(arrays[m + 1 : -1]), arrays[-1]
+    turned = [2, 3, 4]
+    by_row = [slope.shape[1] != param.shape[0] for slope, param in zip(slopes, params)]
+    for at in turned:
+        slopes[at] = slopes[at].transpose(0, 2, 1)
+        params[at] = params[at].T
+        by_row[at] = not by_row[at]
+    f32, bf16 = jnp.float32, jnp.bfloat16
+    halves = [param.shape for param in params]
+    wholes = [slope.shape[1:] for slope in slopes]
+    small = min(half[0] * half[1] for half in halves)
+    chunks = plan(halves, by_row, small)
+    count = len(chunks)
+    width = param_norm.shape[0]
+    dma = pltpu.SemaphoreType.DMA
+    results = sum(rows * columns for rows, columns in wholes) * 2
+    results += sum(rows * columns for rows, columns in halves) * 4
+    outs = pl.pallas_call(
+        functools.partial(exchange, n, by_row, chunks, n ** (-0.5)),
+        out_shape=(
+            *[pltpu.VMEM(whole, bf16) for whole in wholes],
+            pltpu.VMEM((1, n * width), f32),
+            *[pltpu.VMEM(half, f32) for half in halves],
+            pltpu.VMEM((1, width), f32),
+        ),
+        in_specs=[ANY] * (2 * m + 2),
+        out_specs=[pl.BlockSpec(memory_space=pltpu.VMEM)] * (2 * m + 2),
+        scratch_shapes=[
+            *[pltpu.VMEM(half, f32) for half in halves * 2],
+            pltpu.VMEM((n, n * width), f32),
+            pltpu.VMEM((n, width), f32),
+            *[dma((count,))] * 6,
+            *[dma((2,))] * 3,
+        ],
+        compiler_params=pltpu.CompilerParams(
+            collective_id=0, has_side_effects=True, vmem_limit_bytes=VMEM_BYTES - results - 192 * 1024
+        ),
+        name="exchange",
+    )(*slopes, slope_norm, *params, param_norm.reshape(1, width))
+    outs = list(outs)
+    norm_half, norm_next = outs.pop(m), outs.pop()
+    outs = list(pl.pallas_call(
+        functools.partial(settle, 2 * m),
+        out_shape=(
+            *[jax.ShapeDtypeStruct(whole, bf16) for whole in wholes],
+            *[jax.ShapeDtypeStruct(half, f32) for half in halves],
+        ),
+        in_specs=[pl.BlockSpec(memory_space=pltpu.VMEM)] * (2 * m),
+        out_specs=[ANY] * (2 * m),
+        scratch_shapes=[dma((2 * m,))],
+        compiler_params=pltpu.CompilerParams(vmem_limit_bytes=2 * 1024 * 1024),
+        name="settle",
+    )(*outs))
+    for at in turned:
+        outs[at] = outs[at].T
+        outs[m + at] = outs[m + at].T
+    half_norm = norm_half.reshape(n * width).astype(bf16)
+    return (*outs[:m], half_norm, *outs[m:], norm_next.reshape(width))
+
+
+def spread(
     slope_up,
     slope_down,
     slope_query,
@@ -94,8 +305,9 @@
         P(("unit", "model"), "replica"),
         P(("unit", "replica")),
     )
+    n = mesh.shape["replica"]
     return jax.shard_map(
-        shards,
+        functools.partial(shards, n) if n == 2 else spread,
         mesh=mesh,
         in_specs=placed,
         out_specs=(

time: 121 us -> 16.3 us (0.13); the launches traced: 119 us -> 16.1 us
  waiting for transfers between devices: 72.4 us -> 0 us
  between operations: 14.2 us -> 0.66 us
  Pallas kernels: 0 us -> 13 us
  blocking collectives: 12.6 us -> 0 us
  other arithmetic: 12.9 us -> 1.19 us
  local copies, waits for them, and re-layouts: 6.96 us -> 1.25 us
    reduce_scatter x6 -> x0, waiting for transfers between devices: 47.4 us -> none  [the longest x1 11.1 us: shards(): lax.psum_scatter(slope_up[0], 'replica', scatter_dimension=0, tiled=True)]
    all_gather x2 -> x0, waiting for transfers between devices: 21.3 us -> none  [the longest x1 12.5 us: shards(): lax.all_gather(next_down.astype(jnp.bfloat16), 'replica', axis=1, tiled=T...]
    pallas_call x0 -> x2, Pallas kernels: none -> 13 us  [the longest x1 9.97 us: shards(): pl.pallas_call(functools.partial(exchange, n, by_row, chunks, n ** (-0.5)...]
    convert_element_type x7 -> x1, other arithmetic: 12.9 us -> 0.6 us  [shards(): half_norm = norm_half.reshape(n * width).astype(bf16)]
    all_gather x5 -> x0, blocking collectives: 10.1 us -> none  [the longest x1 2.14 us: shards(): lax.all_gather(next_query.astype(jnp.bfloat16), 'replica', axis=0, tiled=...]
    unnamed x26 -> x0, local copies, waits for them, and re-layouts: 6.96 us -> none
    unnamed x8 -> x0, waiting for transfers between devices: 3.66 us -> none
    psum x1 -> x0, blocking collectives: 2.48 us -> none  [shards(): whole_norm = lax.psum(slope_norm[0], 'replica')]
  transfers between devices with their start and end apart: 8 -> 0, of which waited for: 8 -> 0; matrix products, arithmetic and copies ran while one was open for 11% -> 0% of each run, Pallas kernels for 0% -> 0%
where the time goes in v1:
time: 16.3 us; the launch traced here: 16.1 us
  Pallas kernels  13 us (80%)
  local copies, waits for them, and re-layouts  1.25 us (8%)
  other arithmetic  1.19 us (7%)
  between operations  0.66 us (4%)
    pallas_call x1, Pallas kernels, shards(): pl.pallas_call(functools.partial(exchange, n, by_row, chunks, n ** (-0.5)...  9.97 us
    pallas_call x1, Pallas kernels, shards(): pl.pallas_call(functools.partial(settle, 2 * m), out_shape=(*[jax.ShapeDt...  3.01 us
    reshape x1, local copies, waits for them, and re-layouts, shards(): param_norm.reshape(1, width)  1.25 us
    convert_element_type x1, other arithmetic, shards(): half_norm = norm_half.reshape(n * width).astype(bf16)  0.6 us
    pallas_call x1, other arithmetic, shards(): pl.pallas_call(functools.partial(exchange, n, by_row, chunks, n ** (-0.5)...  0.6 us

profile of v1, /device:TPU:3, one launch (start us, length us, event | category | flops | bytes accessed | tf_op | source)
XLA Modules:
  0.0 16.1 jit_solution(15199504136313163348)
XLA Ops:
  0.6 1.2 %reshape.36.refs_13_ = f32[1,384]{1,0:T(1,128)} reshape(f32[384]{0:T(512)} %param.27) | data formatting | bytes 3072 | tf_op jit(solution)/shard_map/reshape | solution.py:198
  1.9 10.0 %exchange.1 = (bf16[768,768]{1,0:T(8,128)(2,1)S(1)}, bf16[768,768]{1,0:T(8,128)(2,1)S(1)}, bf16[192,768]{1,0:T(8,128)(2,1)S(1)}, bf16[192,768]{1,0:T(8,128)(2,1)...) custom-call(f32[1,768,768]{2,1,0:T(8,128)} %refs_0_.1, ...), custom_call_target="tpu_custom_call" | custom-call | tf_op jit(solution)/shard_map/exchange/pallas_call | solution.py:177
  11.9 3.0 %settle.1 = (bf16[768,768]{1,0:T(8,128)(2,1)}, bf16[768,768]{1,0:T(8,128)(2,1)}, bf16[192,768]{1,0:T(8,128)(2,1)}, bf16[192,768]{1,0:T(8,128)(2,1)}, bf16[192,76...) custom-call(bf16[768,768]{1,0:T(8,128)(2,1)S(1)} %get-tuple-element., ...), custom_call_target="tpu_custom_call" | custom-call | tf_op jit(solution)/shard_map/settle/pallas_call | solution.py:201
  14.9 0.6 %convert_reduce_fusion = bf16[768]{0:T(1024)(128)(2,1)} fusion(f32[1,768]{1,0:T(1,128)S(1)} %get-tuple-element.58), kind=kLoop, calls=%fused_computation | loop fusion | flops 768 | bytes 4608 | tf_op jit(solution)/shard_map/convert_element_type | solution.py:216
  15.5 0.6 %reduce.1 = f32[384]{0:T(512)} reduce(f32[1,384]{1,0:T(1,128)S(1)} %get-tuple-element.65, f32[]{:T(128)} %constant.8), dimensions={0}, to_apply=%get-tuple-element.65.reduce_sub_computation | reduce | bytes 3076 | tf_op jit(solution)/shard_map/exchange/pallas_call | solution.py:177

commit v2 on v1

--- a/solution.py
+++ b/solution.py
@@ -36,7 +36,7 @@
     kept, norm_next = refs[m + 1 : 2 * m + 1], refs[2 * m + 1]
     refs = refs[2 * m + 2 :]
     own, got = refs[:m], refs[m : 2 * m]
-    (norms, norm_kept, in_sem, keep_sem, send_sem, recv_sem,
+    (norms, norm_own, norm_got, norm_all, in_sem, keep_sem, send_sem, recv_sem,
      back_send, back_recv, norm_in, norm_send, norm_recv) = refs[2 * m :]
 
     me = lax.axis_index("replica")
@@ -70,7 +70,7 @@
         ))
     norm_loads = (
         pltpu.make_async_copy(slope_norm, norms.at[pl.ds(me, 1)], norm_in.at[0]),
-        pltpu.make_async_copy(param_norm, norm_kept.at[pl.ds(me, 1)], norm_in.at[1]),
+        pltpu.make_async_copy(param_norm, norm_own, norm_in.at[1]),
     )
 
     barrier = pltpu.get_barrier_semaphore()
@@ -79,7 +79,7 @@
 
     norm_sends = [
         remote(slope_norm, norms.at[pl.ds(me, 1)], norm_send.at[0], norm_recv.at[0]),
-        remote(param_norm, norm_kept.at[pl.ds(me, 1)], norm_send.at[1], norm_recv.at[1]),
+        remote(param_norm, norm_got, norm_send.at[1], norm_recv.at[1]),
     ]
     sends = [
         remote(
@@ -124,18 +124,16 @@
         load.wait()
     for send in norm_sends:
         send.wait_recv()
-    width = norm_kept.shape[1]
-    for who in range(n):
-        cut = pl.ds(who * width, width)
-        total = norms[0:1, cut]
-        for other in range(1, n):
-            total += norms[other : other + 1, cut]
-        moved = norm_kept[who : who + 1] - learn_rate * (total * rate)
-        norm_half[0:1, cut] = moved
-
-        @pl.when(who == me)
-        def keep():
-            norm_next[...] = moved
+    width = norm_own.shape[0]
+    total = norms[0:1] + norms[1:2]
+    for where, held in ((me, norm_own), (peer, norm_got)):
+        cut = pl.ds(pl.multiple_of(where * width, width), width)
+        norm_all[0:1, cut] = held[...].reshape(1, width)
+    moved = norm_all[...] - learn_rate * (total * rate)
+    norm_all[...] = moved
+    norm_half[...] = moved.reshape(n * width).astype(jnp.bfloat16)
+    cut = pl.ds(pl.multiple_of(me * width, width), width)
+    norm_next[...] = norm_all[0:1, cut].reshape(width)
 
     for send in sends + norm_sends:
         send.wait_send()
@@ -178,16 +176,18 @@
         functools.partial(exchange, n, by_row, chunks, n ** (-0.5)),
         out_shape=(
             *[pltpu.VMEM(whole, bf16) for whole in wholes],
-            pltpu.VMEM((1, n * width), f32),
+            pltpu.VMEM((n * width,), bf16),
             *[pltpu.VMEM(half, f32) for half in halves],
-            pltpu.VMEM((1, width), f32),
+            pltpu.VMEM((width,), f32),
         ),
         in_specs=[ANY] * (2 * m + 2),
         out_specs=[pl.BlockSpec(memory_space=pltpu.VMEM)] * (2 * m + 2),
         scratch_shapes=[
             *[pltpu.VMEM(half, f32) for half in halves * 2],
             pltpu.VMEM((n, n * width), f32),
-            pltpu.VMEM((n, width), f32),
+            pltpu.VMEM((width,), f32),
+            pltpu.VMEM((width,), f32),
+            pltpu.VMEM((1, n * width), f32),
             *[dma((count,))] * 6,
             *[dma((2,))] * 3,
         ],
@@ -195,26 +195,20 @@
             collective_id=0, has_side_effects=True, vmem_limit_bytes=VMEM_BYTES - results - 192 * 1024
         ),
         name="exchange",
-    )(*slopes, slope_norm, *params, param_norm.reshape(1, width))
-    outs = list(outs)
-    norm_half, norm_next = outs.pop(m), outs.pop()
+    )(*slopes, slope_norm, *params, param_norm)
     outs = list(pl.pallas_call(
-        functools.partial(settle, 2 * m),
-        out_shape=(
-            *[jax.ShapeDtypeStruct(whole, bf16) for whole in wholes],
-            *[jax.ShapeDtypeStruct(half, f32) for half in halves],
-        ),
-        in_specs=[pl.BlockSpec(memory_space=pltpu.VMEM)] * (2 * m),
-        out_specs=[ANY] * (2 * m),
-        scratch_shapes=[dma((2 * m,))],
+        functools.partial(settle, len(outs)),
+        out_shape=[jax.ShapeDtypeStruct(out.shape, out.dtype) for out in outs],
+        in_specs=[pl.BlockSpec(memory_space=pltpu.VMEM)] * len(outs),
+        out_specs=[ANY] * len(outs),
+        scratch_shapes=[dma((len(outs),))],
         compiler_params=pltpu.CompilerParams(vmem_limit_bytes=2 * 1024 * 1024),
         name="settle",
     )(*outs))
     for at in turned:
         outs[at] = outs[at].T
-        outs[m + at] = outs[m + at].T
-    half_norm = norm_half.reshape(n * width).astype(bf16)
-    return (*outs[:m], half_norm, *outs[m:], norm_next.reshape(width))
+        outs[m + 1 + at] = outs[m + 1 + at].T
+    return tuple(outs)
 
 
 def spread(

time: 16.3 us -> 13.9 us (0.85)
  local copies, waits for them, and re-layouts: 1.25 us -> 0 us
  other arithmetic: 1.19 us -> 0 us
    reshape x1 -> x0, local copies, waits for them, and re-layouts: 1.25 us -> none  [shards(): param_norm.reshape(1, width)]
    convert_element_type x1 -> x0, other arithmetic: 0.6 us -> none  [shards(): half_norm = norm_half.reshape(n * width).astype(bf16)]
    pallas_call x1 -> x0, other arithmetic: 0.6 us -> none  [shards(): pl.pallas_call(functools.partial(exchange, n, by_row, chunks, n ** (-0.5)...]
where the time goes in v2:
time: 13.9 us; the launch traced here: 13.7 us
  Pallas kernels  13.1 us (94%)
  between operations  0.66 us (5%)
    pallas_call x1, Pallas kernels, shards(): pl.pallas_call(functools.partial(exchange, n, by_row, chunks, n ** (-0.5)...  10 us
    pallas_call x1, Pallas kernels, shards(): pl.pallas_call(functools.partial(settle, len(outs)), out_shape=[jax.Shape...  3.03 us

profile of v2, /device:TPU:3, one launch (start us, length us, event | category | flops | bytes accessed | tf_op | source)
XLA Modules:
  0.0 13.7 jit_solution(2033443440219442752)
XLA Ops:
  0.7 10.0 %exchange.1 = (bf16[768,768]{1,0:T(8,128)(2,1)S(1)}, bf16[768,768]{1,0:T(8,128)(2,1)S(1)}, bf16[192,768]{1,0:T(8,128)(2,1)S(1)}, bf16[192,768]{1,0:T(8,128)(2,1)...) custom-call(f32[1,768,768]{2,1,0:T(8,128)} %refs_0_.1, ...), custom_call_target="tpu_custom_call" | custom-call | tf_op jit(solution)/shard_map/exchange/pallas_call | solution.py:175
  10.7 3.0 %settle.1 = (bf16[768,768]{1,0:T(8,128)(2,1)}, bf16[768,768]{1,0:T(8,128)(2,1)}, bf16[192,768]{1,0:T(8,128)(2,1)}, bf16[192,768]{1,0:T(8,128)(2,1)}, bf16[192,76...) custom-call(bf16[768,768]{1,0:T(8,128)(2,1)S(1)} %get-tuple-element., ...), custom_call_target="tpu_custom_call" | custom-call | tf_op jit(solution)/shard_map/settle/pallas_call | solution.py:199

commit v3 on v2

--- a/solution.py
+++ b/solution.py
@@ -166,7 +166,7 @@
     halves = [param.shape for param in params]
     wholes = [slope.shape[1:] for slope in slopes]
     small = min(half[0] * half[1] for half in halves)
-    chunks = plan(halves, by_row, small)
+    chunks = plan(halves, by_row, 4 * small)
     count = len(chunks)
     width = param_norm.shape[0]
     dma = pltpu.SemaphoreType.DMA

time: 13.9 us -> 13.6 us (0.978)
  Pallas kernels: 13.1 us -> 12.7 us
    pallas_call x1, Pallas kernels: 10 us -> 9.7 us  [shards(): pl.pallas_call(functools.partial(exchange, n, by_row, chunks, n ** (-0.5)...]
where the time goes in v3:
time: 13.6 us; the launch traced here: 13.4 us
  Pallas kernels  12.7 us (93%)
  between operations  0.66 us (5%)
    pallas_call x1, Pallas kernels, shards(): pl.pallas_call(functools.partial(exchange, n, by_row, chunks, n ** (-0.5)...  9.7 us
    pallas_call x1, Pallas kernels, shards(): pl.pallas_call(functools.partial(settle, len(outs)), out_shape=[jax.Shape...  3.03 us

profile of v3, /device:TPU:3, one launch (start us, length us, event | category | flops | bytes accessed | tf_op | source)
XLA Modules:
  0.0 13.4 jit_solution(7361197397528209399)
XLA Ops:
  0.7 9.7 %exchange.1 = (bf16[768,768]{1,0:T(8,128)(2,1)S(1)}, bf16[768,768]{1,0:T(8,128)(2,1)S(1)}, bf16[192,768]{1,0:T(8,128)(2,1)S(1)}, bf16[192,768]{1,0:T(8,128)(2,1)...) custom-call(f32[1,768,768]{2,1,0:T(8,128)} %refs_0_.1, ...), custom_call_target="tpu_custom_call" | custom-call | tf_op jit(solution)/shard_map/exchange/pallas_call | solution.py:175
  10.4 3.0 %settle.1 = (bf16[768,768]{1,0:T(8,128)(2,1)}, bf16[768,768]{1,0:T(8,128)(2,1)}, bf16[192,768]{1,0:T(8,128)(2,1)}, bf16[192,768]{1,0:T(8,128)(2,1)}, bf16[192,76...) custom-call(bf16[768,768]{1,0:T(8,128)(2,1)S(1)} %get-tuple-element., ...), custom_call_target="tpu_custom_call" | custom-call | tf_op jit(solution)/shard_map/settle/pallas_call | solution.py:199
